TPU v7x, 32 devices: a whole 2x2x4 slice. The times are simulated.
32 devices in a mesh: mem: 2 (over y), lat: 4 (over z), lon: 4 (over x, core).
Axes of the slice: x: 2, y: 2, z: 4, core: 2. Of those that a mesh axis runs over, the one named last changes fastest.
Arguments:
- control: bfloat16 [62, 3, 4, 4, 73728], P('mem', None, 'lat', 'lon'), may hold values from -6 to 6
- perturbs: bfloat16 [62, 3, 4, 4, 73728], P('mem', None, 'lat', 'lon'), may hold values from -0.75 to 0.75
- static_input: bfloat16 [3, 4, 4, 73728], P(None, 'lat', 'lon'), may hold values from -6 to 6
- lat_basis: bfloat16 [768, 384], replicated, may hold values from -0.21875 to 0.21875
- local_spectrum: float32 [384, 768], P(None, 'lat'), may hold values from 0.1 to 1
- static_spectrum: float32 [384, 768], P(None, 'lat'), may hold values from 0.1 to 1
- static_weight: float32 [3], replicated, may hold values from 0.2 to 0.8
Outputs:
- increment: float32 [3, 4, 4, 73728], P(None, 'lat', 'lon')
All inputs are finite; a program needn't handle non-finite values.
Results may differ from a plain program's by a relative error of at most 0.0073.
Values may be sent and summed in bfloat16 or wider, within the bound.
A program may use at most 128 MiB of HBM per device.

v0:
```python
import jax
import jax.numpy as jnp
from jax import lax
from jax.sharding import PartitionSpec as P

NLON = 1536
NLAT = 768
KLON = 768


def zonal_table():
    half = KLON // 2
    points = jnp.arange(NLON, dtype=jnp.int32)
    column = jnp.arange(KLON, dtype=jnp.int32)
    wave = jnp.where(column < half, column, column - half + 1)
    phase = points[:, None] * wave[None, :] % NLON
    angle = 2.0 * jnp.pi / NLON * phase.astype(jnp.float32)
    scale = jnp.sqrt(jnp.float32(2.0 / NLON))
    values = jnp.where(column[None, :] < half, jnp.cos(angle), jnp.sin(angle)) * scale
    return values.astype(jnp.bfloat16)


def shards(
    control, perturbs, static_input, lat_basis, local_spectrum, static_spectrum, static_weight
):
    mem_dev, levels = (control.shape[0], control.shape[1])
    cell_count = control.shape[-1]
    lat_rows = NLAT // lax.axis_size("lat")
    lon_cols = cell_count // lat_rows
    fields = jnp.concatenate([control, static_input[None]], 0).reshape(-1, lat_rows, lon_cols)
    per_lon = fields.shape[0] // lax.axis_size("lon")
    field_index = lax.axis_index("lon") * per_lon + jnp.arange(per_lon, dtype=jnp.int32)
    is_static = field_index >= mem_dev * levels
    first_mem = (lax.axis_index("mem") == 0).astype(jnp.float32)
    zonal = zonal_table()
    strips = lax.all_to_all(fields, "lon", split_axis=0, concat_axis=2, tiled=True)
    waves = jnp.einsum("bxn,nk->kbx", strips, zonal, preferred_element_type=jnp.float32).astype(
        jnp.bfloat16
    )
    merid = lax.all_to_all(waves, "lat", split_axis=0, concat_axis=2, tiled=True)
    coef = jnp.einsum("kby,yj->kbj", merid, lat_basis, preferred_element_type=jnp.float32)
    spectrum = jnp.where(
        is_static[None, :, None], static_spectrum.T[:, None, :], local_spectrum.T[:, None, :]
    )
    scaled = (coef * spectrum).astype(jnp.bfloat16)
    back = jnp.einsum("kbj,yj->kby", scaled, lat_basis, preferred_element_type=jnp.float32).astype(
        jnp.bfloat16
    )
    zonal_rows = lax.all_to_all(back, "lat", split_axis=2, concat_axis=0, tiled=True)
    grid = jnp.einsum("kbx,nk->bxn", zonal_rows, zonal, preferred_element_type=jnp.float32).astype(
        jnp.bfloat16
    )
    pert_fields = perturbs.reshape(mem_dev, levels, lat_rows, lon_cols)
    weight = static_weight[:, None, None]
    filtered = lax.all_to_all(grid, "lon", split_axis=2, concat_axis=0, tiled=True).reshape(
        mem_dev + 1, levels, lat_rows, lon_cols
    )
    ensemble = jnp.einsum(
        "mlxn,mlxn->lxn", pert_fields, filtered[:mem_dev], preferred_element_type=jnp.float32
    )
    static_part = filtered[mem_dev].astype(jnp.float32)
    own = first_mem * weight * static_part + (1.0 - weight) * ensemble
    total = lax.psum(own, "mem")
    return total.reshape(levels, 1, 1, cell_count)


def solution(mesh):
    return jax.shard_map(
        shards,
        mesh=mesh,
        in_specs=(
            P("mem", None, "lat", "lon", None),
            P("mem", None, "lat", "lon", None),
            P(None, "lat", "lon", None),
            P(),
            P(None, "lat"),
            P(None, "lat"),
            P(),
        ),
        out_specs=P(None, "lat", "lon", None),
        check_vma=False,
    )
```

profile of v0, /device:TPU:0, one launch (start us, length us, event | category | flops | bytes accessed | tf_op | source)
XLA Modules:
  0.0 1161.2 jit_solution(15015766370873050855)
XLA Ops:
  6.5 0.0 copy-start
  6.5 1.9 copy.44
  8.4 8.6 pad_maximum_fusion
  17.1 48.5 %copy.45 = bf16[32,3,1,1,73728]{4,1,0,3,2:T(4,128)(2,1)} copy(bf16[32,3,1,1,73728]{4,0,3,2,1:T(8,128)(2,1)S(1)} %pad_maximum_fusion) | data formatting | bytes 28311552 | tf_op jit(solution)/shard_map/concatenate | solution.py:30
  65.6 31.2 %reshape.38 = bf16[96,192,384]{2,1,0:T(8,128)(2,1)} reshape(bf16[32,3,1,1,73728]{4,1,0,3,2:T(4,128)(2,1)} %copy.45) | data formatting | bytes 28311552 | tf_op jit(solution)/shard_map/reshape | solution.py:30
  96.8 6.8 all-to-all-start
  103.7 19.8 %fusion.43 = bf16[1536,768,1]{1,0,2:T(8,128)(2,1)S(1)} fusion(s32[768]{0:T(1024)S(1)} %add_select_fusion.1, pred[768]{0:T(1024)(128)(4,1)S(1)} %iota_compare_fusion), kind=kLoop, calls=%fused_computation.21.clone.1.clone.1 | loop fusion | flops 14155776 | bytes 2363136 | tf_op jit(solution)/shard_map/bxn,nk->kbx/dot_general | solution.py:37
  123.5 135.9 %all-to-all-done = bf16[96,192,384]{2,1,0:T(8,128)(2,1)} async-done(((bf16[96,192,384]{2,1,0:T(8,128)(2,1)}), bf16[96,192,384]{2,1,0:T(8,128)(2,1)}, u32[]{:S(2)}, u32[]{:S(2)}) %all-to-all-start) | async-done | bytes 14155808 | tf_op jit(solution)/shard_map/all_to_all | solution.py:36
  259.4 10.6 copy.62
  270.0 16.3 %convolution_convert_fusion.2 = bf16[768,24,192]{0,2,1:T(8,128)(2,1)} fusion(bf16[24,192,1536]{2,1,0:T(8,128)(2,1)} %bitcast.63, bf16[1536,768,1]{1,0,2:T(8,128)(2,1)S(1)} %fusion.43), kind=kOutput, calls=%fused_computation.10 | convolution fusion | flops 10875174912 | bytes 23592960 | tf_op jit(solution)/shard_map/bxn,nk->kbx/dot_general | solution.py:37
  286.3 13.4 %copy.47 = bf16[768,24,192]{2,1,0:T(8,128)(2,1)} copy(bf16[768,24,192]{0,2,1:T(8,128)(2,1)} %convolution_convert_fusion.2) | data formatting | bytes 14155776 | tf_op jit(solution)/shard_map/convert_element_type | solution.py:37
  299.7 6.3 all-to-all-start.1
  306.1 206.2 %all-to-all-done.1 = bf16[768,24,192]{2,1,0:T(8,128)(2,1)} async-done(((bf16[768,24,192]{2,1,0:T(8,128)(2,1)}), bf16[768,24,192]{2,1,0:T(8,128)(2,1)}, u32[]{:S(2)}, u32[]{:S(2)}) %all-to-all-start.1) | async-done | bytes 7077920 | tf_op jit(solution)/shard_map/all_to_all | solution.py:40
  512.2 20.1 %copy.67 = bf16[4,192,24,192]{3,0,2,1:T(4,128)(2,1)} copy(bf16[4,192,24,192]{3,2,1,0:T(8,128)(2,1)} %bitcast.6) | data formatting | bytes 14155776 | tf_op jit(solution)/shard_map/all_to_all | solution.py:40
  532.3 0.0 copy-start.4
  532.3 0.0 copy-start.5
  532.3 16.6 %all_to_all.57 = bf16[192,24,768]{2,1,0:T(8,128)(2,1)} reshape(bf16[192,24,4,192]{3,2,1,0:T(4,128)(2,1)} %bitcast.61) | data formatting | bytes 14155776 | tf_op jit(solution)/shard_map/all_to_all | solution.py:40
  549.0 0.0 copy-done
  549.0 0.0 copy-done.4
  549.0 0.0 copy-done.5
  549.0 12.1 %convolution_convert_fusion.1 = bf16[192,24,768]{2,1,0:T(8,128)(2,1)} fusion(f32[192,384]{1,0:T(8,128)S(1)} %bitcast.65, f32[192,384]{1,0:T(8,128)S(1)} %bitcast.66, pred[24]{0:T(512)(128)(4,1)S(1)} %add_compare_fusion, bf16[192,24,768]{2,1,0:T(8,128)(2,1)} %all_to_all.57, bf16[768,384]{1,0:T(8,128)(2,1)S(1)} %copy-done), kind=kOutput, calls=%fused_computation.9 | convolution fusion | flops 5444665344 | bytes 15335448 | tf_op jit(solution)/shard_map/kbj,yj->kby/dot_general | solution.py:46
  561.1 13.5 %copy.49 = bf16[192,24,768]{0,1,2:T(8,128)(2,1)} copy(bf16[192,24,768]{2,1,0:T(8,128)(2,1)} %convolution_convert_fusion.1) | data formatting | bytes 14155776 | tf_op jit(solution)/shard_map/convert_element_type | solution.py:46
  574.6 6.0 all-to-all-start.2
  580.6 19.8 %fusion.41 = bf16[1536,768,1]{1,0,2:T(8,128)(2,1)S(1)} fusion(s32[768]{0:T(1024)S(1)} %add_select_fusion.1, pred[768]{0:T(1024)(128)(4,1)S(1)} %iota_compare_fusion), kind=kLoop, calls=%fused_computation.21.clone.clone.1 | loop fusion | flops 14155776 | bytes 2363136 | tf_op jit(solution)/shard_map/kbx,nk->bxn/dot_general | solution.py:50
  600.4 185.1 %all-to-all-done.2 = bf16[192,24,768]{0,1,2:T(8,128)(2,1)} async-done(((bf16[192,24,768]{0,1,2:T(8,128)(2,1)}), bf16[192,24,768]{0,1,2:T(8,128)(2,1)}, u32[]{:S(2)}, u32[]{:S(2)}) %all-to-all-start.2) | async-done | bytes 7077920 | tf_op jit(solution)/shard_map/all_to_all | solution.py:49
  785.5 13.5 %copy.66 = bf16[192,24,4,192]{0,2,3,1:T(4,128)(2,1)} copy(bf16[192,24,4,192]{0,1,3,2:T(8,128)(2,1)} %bitcast.11) | data formatting | bytes 14155776 | tf_op jit(solution)/shard_map/all_to_all | solution.py:49
  799.0 16.6 %all_to_all.61 = bf16[768,24,192]{0,2,1:T(8,128)(2,1)} reshape(bf16[4,192,24,192]{1,0,3,2:T(4,128)(2,1)} %bitcast.62) | data formatting | bytes 14155776 | tf_op jit(solution)/shard_map/all_to_all | solution.py:49
  815.6 16.9 %convolution_convert_fusion = bf16[24,192,1536]{2,1,0:T(8,128)(2,1)} fusion(bf16[768,24,192]{0,2,1:T(8,128)(2,1)} %all_to_all.61, bf16[1536,768,1]{1,0,2:T(8,128)(2,1)S(1)} %fusion.41), kind=kOutput, calls=%fused_computation.2 | convolution fusion | flops 10878713856 | bytes 23592960 | tf_op jit(solution)/shard_map/kbx,nk->bxn/dot_general | solution.py:50
  832.5 26.0 %copy.51 = bf16[24,192,1536]{1,0,2:T(8,128)(2,1)} copy(bf16[24,192,1536]{2,1,0:T(8,128)(2,1)} %convolution_convert_fusion) | data formatting | bytes 28311552 | tf_op jit(solution)/shard_map/convert_element_type | solution.py:50
  858.6 7.3 all-to-all-start.3
  865.9 0.0 copy-start.3
  865.9 0.3 all-reduce.2.cloned.1.call-start
  866.2 22.7 %reshape.40 = bf16[31,3,192,384]{3,2,0,1:T(8,128)(2,1)} reshape(bf16[31,3,1,1,73728]{4,0,3,2,1:T(8,128)(2,1)} %param.8) | data formatting | bytes 27426816 | tf_op jit(solution)/shard_map/reshape | solution.py:53
  888.9 0.0 copy-done.3
  889.0 182.5 %all-to-all-done.3 = bf16[24,192,1536]{1,0,2:T(8,128)(2,1)} async-done(((bf16[24,192,1536]{1,0,2:T(8,128)(2,1)}), bf16[24,192,1536]{1,0,2:T(8,128)(2,1)}, u32[]{:S(2)}, u32[]{:S(2)}) %all-to-all-start.3) | async-done | bytes 14155808 | tf_op jit(solution)/shard_map/all_to_all | solution.py:55
  1071.4 23.4 %copy.61 = bf16[24,192,4,384]{3,2,1,0:T(4,128)(2,1)} copy(bf16[24,192,4,384]{1,0,3,2:T(8,128)(2,1)} %bitcast.13) | data formatting | bytes 28311552 | tf_op jit(solution)/shard_map/all_to_all | solution.py:55
  1094.8 0.0 copy-start.2
  1094.8 8.5 copy.53
  1103.3 0.6 copy-done.2
  1103.9 0.0 copy-start.1
  1103.9 4.1 multiply_reduce_fusion
  1108.1 0.2 fusion.20
  1108.3 1.5 reshape.41
  1109.7 0.0 all-reduce.2.cloned.1.call-update
  1109.8 41.3 %all-reduce.2.cloned.1.call-done = f32[3,1,1,73728]{3,0,2,1:T(4,128)} async-done(((f32[3,1,1,73728]{3,0,2,1:T(4,128)}), f32[3,1,1,73728]{3,0,2,1:T(4,128)}) %all-reduce.2.cloned.1.call-update) | async-done | bytes 884752 | tf_op jit(solution)/shard_map/psum | solution.py:63
  1151.0 3.1 copy.54
  1154.1 0.0 copy-done.1
  (4 shorter events, 0.0 us)
Async XLA Ops:
  6.5 542.4 %copy-start = (bf16[768,384]{1,0:T(8,128)(2,1)S(1)}, bf16[768,384]{1,0:T(8,128)(2,1)}, u32[]{:S(2)}) copy-start(bf16[768,384]{1,0:T(8,128)(2,1)} %param.10) | copy-start | bytes 1769476
  96.8 162.6 %all-to-all-start = ((bf16[96,192,384]{2,1,0:T(8,128)(2,1)}), bf16[96,192,384]{2,1,0:T(8,128)(2,1)}, u32[]{:S(2)}, u32[]{:S(2)}) async-start(bf16[96,192,384]{2,1,0:T(8,128)(2,1)} %reshape.38), calls=%async_computation | async-start | bytes 28311552 | tf_op jit(solution)/shard_map/all_to_all | solution.py:36
  299.7 212.5 %all-to-all-start.1 = ((bf16[768,24,192]{2,1,0:T(8,128)(2,1)}), bf16[768,24,192]{2,1,0:T(8,128)(2,1)}, u32[]{:S(2)}, u32[]{:S(2)}) async-start(bf16[768,24,192]{2,1,0:T(8,128)(2,1)} %copy.47), calls=%async_computation.1 | async-start | bytes 18874368 | tf_op jit(solution)/shard_map/all_to_all | solution.py:40
  532.3 16.6 %copy-start.4 = (f32[384,192]{0,1:T(8,128)S(1)}, f32[384,192]{0,1:T(8,128)}, u32[]{:S(2)}) copy-start(f32[384,192]{0,1:T(8,128)} %param.11) | copy-start | bytes 884740
  532.3 16.6 %copy-start.5 = (f32[384,192]{0,1:T(8,128)S(1)}, f32[384,192]{0,1:T(8,128)}, u32[]{:S(2)}) copy-start(f32[384,192]{0,1:T(8,128)} %param.12) | copy-start | bytes 884740
  574.6 210.9 %all-to-all-start.2 = ((bf16[192,24,768]{0,1,2:T(8,128)(2,1)}), bf16[192,24,768]{0,1,2:T(8,128)(2,1)}, u32[]{:S(2)}, u32[]{:S(2)}) async-start(bf16[192,24,768]{0,1,2:T(8,128)(2,1)} %copy.49), calls=%async_computation.2 | async-start | bytes 18874368 | tf_op jit(solution)/shard_map/all_to_all | solution.py:49
  858.6 212.9 %all-to-all-start.3 = ((bf16[24,192,1536]{1,0,2:T(8,128)(2,1)}), bf16[24,192,1536]{1,0,2:T(8,128)(2,1)}, u32[]{:S(2)}, u32[]{:S(2)}) async-start(bf16[24,192,1536]{1,0,2:T(8,128)(2,1)} %copy.51), calls=%async_computation.3 | async-start | bytes 37748736 | tf_op jit(solution)/shard_map/all_to_all | solution.py:55
  865.9 23.0 %copy-start.3 = (f32[3]{0:T(128)S(1)}, f32[3]{0:T(128)}, u32[]{:S(2)}) copy-start(f32[3]{0:T(128)} %param.13) | copy-start | bytes 40
  865.9 285.1 %all-reduce.2.cloned.1.call-start = ((), (), s32[]{:S(2)}) async-start(), calls=%async_computation.4 | async-start | bytes 2359296 | tf_op jit(solution)/shard_map/psum | solution.py:63
  1094.8 9.2 copy-start.2
  1103.9 50.2 %copy-start.1 = (bf16[768,384]{1,0:T(8,128)(2,1)S(1)}, bf16[768,384]{1,0:T(8,128)(2,1)}, u32[]{:S(2)}) copy-start(bf16[768,384]{1,0:T(8,128)(2,1)} %param.10) | copy-start | bytes 1769476
Sparse Core Ops, SparseCore 0:
  1109.9 41.1 all-reduce.1
where the time goes:
time: 1170 us; the launch traced here: 1160 us
  waiting for transfers between devices  751 us (64%)
  local copies, waits for them, and re-layouts  272 us (23%)
  other arithmetic  52.6 us (4%)
  matrix products  45.4 us (4%)
  starting transfers between devices  26.8 us (2%)
  between operations  13.8 us (1%)
    all_to_all x1, waiting for transfers between devices, shards(): lax.all_to_all(waves, 'lat', split_axis=0, concat_axis=2, tiled=True)  206 us
    all_to_all x1, waiting for transfers between devices, shards(): lax.all_to_all(back, 'lat', split_axis=2, concat_axis=0, tiled=True)  185 us
    all_to_all x1, waiting for transfers between devices, shards(): lax.all_to_all(grid, 'lon', split_axis=2, concat_axis=0, tiled=True)  182 us
    all_to_all x1, waiting for transfers between devices, shards(): lax.all_to_all(fields, 'lon', split_axis=0, concat_axis=2, tiled=True)  136 us
    concatenate x1, local copies, waits for them, and re-layouts, shards(): jnp.concatenate([control, static_input[None]], 0)  48.5 us
    psum x1, waiting for transfers between devices, shards(): total = lax.psum(own, 'mem')  41.3 us
    all_to_all x2, local copies, waits for them, and re-layouts, shards(): lax.all_to_all(waves, 'lat', split_axis=0, concat_axis=2, tiled=True)  36.7 us
    all_to_all x2, local copies, waits for them, and re-layouts, shards(): lax.all_to_all(grid, 'lon', split_axis=2, concat_axis=0, tiled=True)  31.9 us
  transfers between devices with their start and end apart: 5, of which 5 were waited for; matrix products, arithmetic and copies ran while one was open for 5% of the time, Pallas kernels for 0%

commit v1 on v0

--- a/solution.py
+++ b/solution.py
@@ -52,9 +52,10 @@
     )
     pert_fields = perturbs.reshape(mem_dev, levels, lat_rows, lon_cols)
     weight = static_weight[:, None, None]
-    filtered = lax.all_to_all(grid, "lon", split_axis=2, concat_axis=0, tiled=True).reshape(
-        mem_dev + 1, levels, lat_rows, lon_cols
-    )
+    filtered = jnp.concatenate(
+        lax.all_to_all(jnp.stack(jnp.split(grid, lax.axis_size("lon"), axis=2)), "lon", 0, 0),
+        axis=0,
+    ).reshape(mem_dev + 1, levels, lat_rows, lon_cols)
     ensemble = jnp.einsum(
         "mlxn,mlxn->lxn", pert_fields, filtered[:mem_dev], preferred_element_type=jnp.float32
     )

time: 1170 us -> 1070 us (0.915)
  waiting for transfers between devices: 751 us -> 693 us
  local copies, waits for them, and re-layouts: 272 us -> 219 us
  other arithmetic: 52.6 us -> 65.5 us
    all_to_all x1, waiting for transfers between devices: 182 us -> 132 us  [shards(): lax.all_to_all(jnp.stack(jnp.split(grid, lax.axis_size('lon'), axis=2)),...]
    all_to_all x2 -> x0, local copies, waits for them, and re-layouts: 31.9 us -> none  [shards(): lax.all_to_all(grid, 'lon', split_axis=2, concat_axis=0, tiled=True)]
    convert_element_type x1 -> x0, local copies, waits for them, and re-layouts: 26 us -> none  [shards(): jnp.einsum('kbx,nk->bxn', zonal_rows, zonal, preferred_element_type=jnp.f...]
  transfers between devices with their start and end apart: 5 -> 5, of which waited for: 5 -> 5; matrix products, arithmetic and copies ran while one was open for 5% -> 6% of each run, Pallas kernels for 0% -> 0%
where the time goes in v1:
time: 1070 us; the launch traced here: 1060 us
  waiting for transfers between devices  693 us (65%)
  local copies, waits for them, and re-layouts  219 us (20%)
  other arithmetic  65.5 us (6%)
  matrix products  45.3 us (4%)
  starting transfers between devices  25.7 us (2%)
  between operations  13.5 us (1%)
    all_to_all x1, waiting for transfers between devices, shards(): lax.all_to_all(waves, 'lat', split_axis=0, concat_axis=2, tiled=True)  206 us
    all_to_all x1, waiting for transfers between devices, shards(): lax.all_to_all(back, 'lat', split_axis=2, concat_axis=0, tiled=True)  185 us
    all_to_all x1, waiting for transfers between devices, shards(): lax.all_to_all(fields, 'lon', split_axis=0, concat_axis=2, tiled=True)  136 us
    all_to_all x1, waiting for transfers between devices, shards(): lax.all_to_all(jnp.stack(jnp.split(grid, lax.axis_size('lon'), axis=2)),...  132 us
    concatenate x1, local copies, waits for them, and re-layouts, shards(): jnp.concatenate([control, static_input[None]], 0)  48.5 us
    all_to_all x2, local copies, waits for them, and re-layouts, shards(): lax.all_to_all(waves, 'lat', split_axis=0, concat_axis=2, tiled=True)  36.7 us
    psum x1, waiting for transfers between devices, shards(): total = lax.psum(own, 'mem')  34.8 us
    reshape x1, local copies, waits for them, and re-layouts, shards(): jnp.concatenate([control, static_input[None]], 0)  31.2 us
  transfers between devices with their start and end apart: 5, of which 5 were waited for; matrix products, arithmetic and copies ran while one was open for 6% of the time, Pallas kernels for 0%

profile of v1, /device:TPU:0, one launch (start us, length us, event | category | flops | bytes accessed | tf_op | source)
XLA Modules:
  0.0 1062.5 jit_solution(9279485750616114646)
XLA Ops:
  6.5 0.0 copy-start
  6.5 1.9 copy.22
  8.4 8.6 pad_maximum_fusion
  17.1 48.5 %copy.23 = bf16[32,3,1,1,73728]{4,1,0,3,2:T(4,128)(2,1)} copy(bf16[32,3,1,1,73728]{4,0,3,2,1:T(8,128)(2,1)S(1)} %pad_maximum_fusion) | data formatting | bytes 28311552 | tf_op jit(solution)/shard_map/concatenate | solution.py:30
  65.6 31.2 %reshape.34 = bf16[96,192,384]{2,1,0:T(8,128)(2,1)} reshape(bf16[32,3,1,1,73728]{4,1,0,3,2:T(4,128)(2,1)} %copy.23) | data formatting | bytes 28311552 | tf_op jit(solution)/shard_map/reshape | solution.py:30
  96.8 6.7 all-to-all-start
  103.6 19.8 %fusion.43 = bf16[1536,768,1]{1,0,2:T(8,128)(2,1)S(1)} fusion(s32[768]{0:T(1024)S(1)} %add_select_fusion.1, pred[768]{0:T(1024)(128)(4,1)S(1)} %iota_compare_fusion), kind=kLoop, calls=%fused_computation.26.clone.1.clone.1 | loop fusion | flops 14155776 | bytes 2363136 | tf_op jit(solution)/shard_map/bxn,nk->kbx/dot_general | solution.py:37
  123.4 135.9 %all-to-all-done = bf16[96,192,384]{2,1,0:T(8,128)(2,1)} async-done(((bf16[96,192,384]{2,1,0:T(8,128)(2,1)}), bf16[96,192,384]{2,1,0:T(8,128)(2,1)}, u32[]{:S(2)}, u32[]{:S(2)}) %all-to-all-start) | async-done | bytes 14155808 | tf_op jit(solution)/shard_map/all_to_all | solution.py:36
  259.3 10.6 %copy.35 = bf16[4,24,24,8,384]{4,3,0,2,1:T(8,128)(2,1)} copy(bf16[4,24,24,8,384]{4,3,2,1,0:T(8,128)(2,1)} %bitcast.21) | data formatting | bytes 28311552 | tf_op jit(solution)/shard_map/all_to_all | solution.py:36
  269.9 16.3 %convolution_convert_fusion.2 = bf16[768,24,192]{0,2,1:T(8,128)(2,1)} fusion(bf16[24,192,1536]{2,1,0:T(8,128)(2,1)} %bitcast.66, bf16[1536,768,1]{1,0,2:T(8,128)(2,1)S(1)} %fusion.43), kind=kOutput, calls=%fused_computation.11 | convolution fusion | flops 10875174912 | bytes 23592960 | tf_op jit(solution)/shard_map/bxn,nk->kbx/dot_general | solution.py:37
  286.2 13.4 %copy.25 = bf16[768,24,192]{2,1,0:T(8,128)(2,1)} copy(bf16[768,24,192]{0,2,1:T(8,128)(2,1)} %convolution_convert_fusion.2) | data formatting | bytes 14155776 | tf_op jit(solution)/shard_map/convert_element_type | solution.py:37
  299.6 6.0 all-to-all-start.1
  305.7 206.0 %all-to-all-done.1 = bf16[768,24,192]{2,1,0:T(8,128)(2,1)} async-done(((bf16[768,24,192]{2,1,0:T(8,128)(2,1)}), bf16[768,24,192]{2,1,0:T(8,128)(2,1)}, u32[]{:S(2)}, u32[]{:S(2)}) %all-to-all-start.1) | async-done | bytes 7077920 | tf_op jit(solution)/shard_map/all_to_all | solution.py:40
  511.7 20.1 %copy.40 = bf16[4,192,24,192]{3,0,2,1:T(4,128)(2,1)} copy(bf16[4,192,24,192]{3,2,1,0:T(8,128)(2,1)} %bitcast.6) | data formatting | bytes 14155776 | tf_op jit(solution)/shard_map/all_to_all | solution.py:40
  531.8 0.0 copy-start.3
  531.8 0.0 copy-start.4
  531.8 16.6 %all_to_all.49 = bf16[192,24,768]{2,1,0:T(8,128)(2,1)} reshape(bf16[192,24,4,192]{3,2,1,0:T(4,128)(2,1)} %bitcast.64) | data formatting | bytes 14155776 | tf_op jit(solution)/shard_map/all_to_all | solution.py:40
  548.4 0.0 copy-done
  548.4 0.0 copy-done.3
  548.4 0.0 copy-done.4
  548.4 12.1 %convolution_convert_fusion.1 = bf16[192,24,768]{2,1,0:T(8,128)(2,1)} fusion(f32[192,384]{1,0:T(8,128)S(1)} %bitcast.68, f32[192,384]{1,0:T(8,128)S(1)} %bitcast.69, pred[24]{0:T(512)(128)(4,1)S(1)} %add_compare_fusion, bf16[192,24,768]{2,1,0:T(8,128)(2,1)} %all_to_all.49, bf16[768,384]{1,0:T(8,128)(2,1)S(1)} %copy-done), kind=kOutput, calls=%fused_computation.10 | convolution fusion | flops 5444665344 | bytes 15335448 | tf_op jit(solution)/shard_map/kbj,yj->kby/dot_general | solution.py:46
  560.5 13.5 %copy.27 = bf16[192,24,768]{0,1,2:T(8,128)(2,1)} copy(bf16[192,24,768]{2,1,0:T(8,128)(2,1)} %convolution_convert_fusion.1) | data formatting | bytes 14155776 | tf_op jit(solution)/shard_map/convert_element_type | solution.py:46
  574.0 6.1 all-to-all-start.2
  580.1 19.8 %fusion.41 = bf16[1536,768,1]{1,0,2:T(8,128)(2,1)S(1)} fusion(s32[768]{0:T(1024)S(1)} %add_select_fusion.1, pred[768]{0:T(1024)(128)(4,1)S(1)} %iota_compare_fusion), kind=kLoop, calls=%fused_computation.26.clone.clone.1 | loop fusion | flops 14155776 | bytes 2363136 | tf_op jit(solution)/shard_map/kbx,nk->bxn/dot_general | solution.py:50
  599.9 184.9 %all-to-all-done.2 = bf16[192,24,768]{0,1,2:T(8,128)(2,1)} async-done(((bf16[192,24,768]{0,1,2:T(8,128)(2,1)}), bf16[192,24,768]{0,1,2:T(8,128)(2,1)}, u32[]{:S(2)}, u32[]{:S(2)}) %all-to-all-start.2) | async-done | bytes 7077920 | tf_op jit(solution)/shard_map/all_to_all | solution.py:49
  784.8 13.5 %copy.39 = bf16[192,24,4,192]{0,2,3,1:T(4,128)(2,1)} copy(bf16[192,24,4,192]{0,1,3,2:T(8,128)(2,1)} %bitcast.11) | data formatting | bytes 14155776 | tf_op jit(solution)/shard_map/all_to_all | solution.py:49
  798.3 16.6 %all_to_all.53 = bf16[768,24,192]{0,2,1:T(8,128)(2,1)} reshape(bf16[4,192,24,192]{1,0,3,2:T(4,128)(2,1)} %bitcast.65) | data formatting | bytes 14155776 | tf_op jit(solution)/shard_map/all_to_all | solution.py:49
  814.8 16.9 %convolution_convert_fusion = bf16[24,192,1536]{2,1,0:T(8,128)(2,1)} fusion(bf16[768,24,192]{0,2,1:T(8,128)(2,1)} %all_to_all.53, bf16[1536,768,1]{1,0,2:T(8,128)(2,1)S(1)} %fusion.41), kind=kOutput, calls=%fused_computation.3 | convolution fusion | flops 10878713856 | bytes 23592960 | tf_op jit(solution)/shard_map/kbx,nk->bxn/dot_general | solution.py:50
  831.8 6.1 slice_bitcast_fusion.4
  837.9 5.3 pad_maximum_fusion.1
  843.2 6.6 all-to-all-start.3
  849.8 0.0 copy-start.2
  849.8 0.3 all-reduce.2.cloned.1.call-start
  850.1 22.8 %reshape.35 = bf16[31,3,192,384]{3,2,0,1:T(8,128)(2,1)} reshape(bf16[31,3,1,1,73728]{4,0,3,2,1:T(8,128)(2,1)} %param.8) | data formatting | bytes 27426816 | tf_op jit(solution)/shard_map/reshape | solution.py:53
  872.9 0.0 copy-done.2
  872.9 131.8 %all-to-all-done.3 = bf16[4,24,192,384]{3,2,1,0:T(8,128)(2,1)} async-done(((bf16[4,24,192,384]{3,2,1,0:T(8,128)(2,1)}), bf16[4,24,192,384]{3,2,1,0:T(8,128)(2,1)}, u32[]{:S(2)}, u32[]{:S(2)}) %all-to-all-start.3) | async-done | bytes 14155808 | tf_op jit(solution)/shard_map/all_to_all | solution.py:56
  1004.7 0.0 copy-start.1
  1004.7 10.7 %multiply_reduce_fusion = f32[3,192,384]{2,1,0:T(8,128)S(1)} fusion(bf16[31,3,192,384]{3,2,0,1:T(8,128)(2,1)} %reshape.35, bf16[32,3,192,384]{3,2,1,0:T(8,128)(2,1)} %bitcast.17), kind=kLoop, calls=%fused_computation | loop fusion | flops 27205632 | bytes 28311552 | tf_op jit(solution)/shard_map/mlxn,mlxn->lxn/dot_general | solution.py:59
  1015.4 1.2 fusion.20
  1016.6 2.0 reshape.36
  1018.6 0.0 all-reduce.2.cloned.1.call-update
  1018.7 34.8 %all-reduce.2.cloned.1.call-done = f32[3,1,1,73728]{3,2,1,0:T(1,128)} async-done(((f32[3,1,1,73728]{3,2,1,0:T(1,128)}), f32[3,1,1,73728]{3,2,1,0:T(1,128)}) %all-reduce.2.cloned.1.call-update) | async-done | bytes 884752 | tf_op jit(solution)/shard_map/psum | solution.py:64
  1053.5 2.1 copy.42
  1055.6 0.0 copy-done.1
  (4 shorter events, 0.0 us)
Async XLA Ops:
  6.5 541.9 %copy-start = (bf16[768,384]{1,0:T(8,128)(2,1)S(1)}, bf16[768,384]{1,0:T(8,128)(2,1)}, u32[]{:S(2)}) copy-start(bf16[768,384]{1,0:T(8,128)(2,1)} %param.10) | copy-start | bytes 1769476
  96.8 162.5 %all-to-all-start = ((bf16[96,192,384]{2,1,0:T(8,128)(2,1)}), bf16[96,192,384]{2,1,0:T(8,128)(2,1)}, u32[]{:S(2)}, u32[]{:S(2)}) async-start(bf16[96,192,384]{2,1,0:T(8,128)(2,1)} %reshape.34), calls=%async_computation | async-start | bytes 28311552 | tf_op jit(solution)/shard_map/all_to_all | solution.py:36
  299.6 212.1 %all-to-all-start.1 = ((bf16[768,24,192]{2,1,0:T(8,128)(2,1)}), bf16[768,24,192]{2,1,0:T(8,128)(2,1)}, u32[]{:S(2)}, u32[]{:S(2)}) async-start(bf16[768,24,192]{2,1,0:T(8,128)(2,1)} %copy.25), calls=%async_computation.1 | async-start | bytes 18874368 | tf_op jit(solution)/shard_map/all_to_all | solution.py:40
  531.8 16.6 %copy-start.3 = (f32[384,192]{0,1:T(8,128)S(1)}, f32[384,192]{0,1:T(8,128)}, u32[]{:S(2)}) copy-start(f32[384,192]{0,1:T(8,128)} %param.11) | copy-start | bytes 884740
  531.8 16.6 %copy-start.4 = (f32[384,192]{0,1:T(8,128)S(1)}, f32[384,192]{0,1:T(8,128)}, u32[]{:S(2)}) copy-start(f32[384,192]{0,1:T(8,128)} %param.12) | copy-start | bytes 884740
  574.0 210.8 %all-to-all-start.2 = ((bf16[192,24,768]{0,1,2:T(8,128)(2,1)}), bf16[192,24,768]{0,1,2:T(8,128)(2,1)}, u32[]{:S(2)}, u32[]{:S(2)}) async-start(bf16[192,24,768]{0,1,2:T(8,128)(2,1)} %copy.27), calls=%async_computation.2 | async-start | bytes 18874368 | tf_op jit(solution)/shard_map/all_to_all | solution.py:49
  843.2 161.5 %all-to-all-start.3 = ((bf16[4,24,192,384]{3,2,1,0:T(8,128)(2,1)}), bf16[4,24,192,384]{3,2,1,0:T(8,128)(2,1)}, u32[]{:S(2)}, u32[]{:S(2)}) async-start(bf16[4,24,192,384]{3,2,1,0:T(8,128)(2,1)} %pad_maximum_fusion.1), calls=%async_computation.3 | async-start | bytes 28311552 | tf_op jit(solution)/shard_map/all_to_all | solution.py:56
  849.8 23.1 %copy-start.2 = (f32[3]{0:T(128)S(1)}, f32[3]{0:T(128)}, u32[]{:S(2)}) copy-start(f32[3]{0:T(128)} %param.13) | copy-start | bytes 40
  849.8 203.7 %all-reduce.2.cloned.1.call-start = ((), (), s32[]{:S(2)}) async-start(), calls=%async_computation.4 | async-start | bytes 1769472 | tf_op jit(solution)/shard_map/psum | solution.py:64
  1004.7 50.9 %copy-start.1 = (bf16[768,384]{1,0:T(8,128)(2,1)S(1)}, bf16[768,384]{1,0:T(8,128)(2,1)}, u32[]{:S(2)}) copy-start(bf16[768,384]{1,0:T(8,128)(2,1)} %param.10) | copy-start | bytes 1769476
Sparse Core Ops, SparseCore 0:
  1018.8 34.6 all-reduce.1
